TPU v7x, 256 devices: a whole 4x4x8 slice. The times are simulated.
256 devices in a mesh: wide: 32 (over x, y, core), narrow: 8 (over z).
Axes of the slice: x: 4, y: 4, z: 8, core: 2. Of those that a mesh axis runs over, the one named last changes fastest.
Arguments:
- row_vectors: bfloat16 [32768, 2048], P('wide'), may hold values from -0.59765625 to 1.3984375
- col_vectors: bfloat16 [4096, 2048], P('narrow', 'wide'), may hold values from -0.59765625 to 1.3984375
- primal_matrix: bfloat16 [2048, 2048], P('wide'), may hold values from -1 to 3, as said below
- dual_inverse: bfloat16 [2048, 2048], P('wide'), may hold values from -1 to 3, as said below
Outputs:
- factored: float32 [32768, 4096], P('wide', 'narrow')
Inputs may be any that keep to these rules, and one draw needn't show every extreme that they name: `primal_matrix`: symmetric positive definite. `dual_inverse`: symmetric positive definite.
All inputs are finite; a program needn't handle non-finite values.
Results may differ from a plain program's by a relative error of at most 0.0027.
Values may be sent and summed in bfloat16 or wider, within the bound.
A program may use at most 64 MiB of HBM per device.

v0:
```python
import jax
import jax.numpy as jnp
from jax import lax
from jax.sharding import PartitionSpec as P


def from_everyone(x, axis):
    devices = lax.axis_size(axis)
    return lax.all_to_all(jnp.broadcast_to(x[None], (devices, *x.shape)), axis, 0, 0, tiled=True)


def joined_along(tiles, dim):
    shape = list(tiles.shape[1:])
    shape[dim] *= tiles.shape[0]
    return jnp.moveaxis(tiles, 0, dim).reshape(shape)


def gather_directly(x, axis, dim):
    tiles = from_everyone(x, axis)
    return joined_along(tiles, dim)


def broadcast(x, axis, root):
    return lax.dynamic_index_in_dim(lax.all_gather(x, axis), root, 0, keepdims=False)


def in_one_piece(arrays, axis, dim, along):
    both = jnp.concatenate(arrays, axis=along)
    whole, at, finished = (lax.all_gather(both, axis, axis=dim, tiled=True), 0, [])
    for a in arrays:
        finished.append(lax.slice_in_dim(whole, at, at + a.shape[along], axis=along))
        at += a.shape[along]
    return tuple(finished)


def spread(value, axis, source):
    kept = jnp.where(lax.axis_index(axis) == source, value, 0).astype(value.dtype)
    return lax.psum(kept, axis)


def per_device(row_vectors, col_vectors, primal_matrix, dual_inverse):
    wide_count = lax.axis_size("wide")
    wide_index = lax.axis_index("wide")
    narrow_index = lax.axis_index("narrow")
    cone_order = primal_matrix.shape[1]
    panel_width = col_vectors.shape[0]
    panel_share = panel_width // wide_count
    gram_scale = 16.0 / (cone_order * cone_order)
    column_set = gather_directly(col_vectors, "wide", 1)
    local_panel = lax.dynamic_slice_in_dim(column_set, wide_index * panel_share, panel_share, 0)
    panel_set = broadcast(local_panel, "narrow", 0)
    prod_primal = jnp.dot(primal_matrix, column_set.T, preferred_element_type=jnp.float32).astype(
        jnp.bfloat16
    )
    prod_dual = jnp.dot(dual_inverse, column_set.T, preferred_element_type=jnp.float32).astype(
        jnp.bfloat16
    )
    pieces = in_one_piece((prod_primal, prod_dual), "wide", 0, 1)
    row_slice = row_vectors
    panel_slice = panel_set
    gram_primal = jnp.dot(row_slice, pieces[0], preferred_element_type=jnp.float32)
    gram_dual = jnp.dot(row_slice, pieces[1], preferred_element_type=jnp.float32)
    tile_primal = jnp.dot(panel_slice, pieces[0], preferred_element_type=jnp.float32)
    tile_dual = jnp.dot(panel_slice, pieces[1], preferred_element_type=jnp.float32)
    slab = gram_primal * gram_dual * gram_scale
    panel_tile = tile_primal * tile_dual * gram_scale
    gram = gather_directly(panel_tile, "wide", 0)
    panel_primal, panel_dual = (spread(prod_primal, "narrow", 0), spread(prod_dual, "narrow", 0))
    pieces = in_one_piece((panel_primal, panel_dual), "wide", 0, 1)
    row_slice = row_vectors
    panel_slice = panel_set
    first_primal = jnp.dot(row_slice, pieces[0], preferred_element_type=jnp.float32)
    first_dual = jnp.dot(row_slice, pieces[1], preferred_element_type=jnp.float32)
    diag_primal = jnp.dot(panel_slice, pieces[0], preferred_element_type=jnp.float32)
    diag_dual = jnp.dot(panel_slice, pieces[1], preferred_element_type=jnp.float32)
    slab_first = first_primal * first_dual * gram_scale
    diag_share = diag_primal * diag_dual * gram_scale
    diag_block = gather_directly(diag_share, "wide", 0)
    factor = jnp.linalg.cholesky(diag_block)
    panel_cols = jax.scipy.linalg.solve_triangular(factor, slab_first.T, lower=True).T
    solved = jax.scipy.linalg.solve_triangular(factor, gram, lower=True)
    trailing = slab - jnp.dot(panel_cols, solved, precision=lax.Precision.HIGHEST)
    return jnp.where(narrow_index == 0, panel_cols, trailing)


def solution(mesh):
    placed = (P("wide", None), P("narrow", "wide"), P("wide", None), P("wide", None))
    return jax.shard_map(
        per_device, mesh=mesh, in_specs=placed, out_specs=P("wide", "narrow"), check_vma=False
    )
```

profile of v0, /device:TPU:1, one launch (start us, length us, event | category | flops | bytes accessed | tf_op | source)
XLA Modules:
  0.0 366.3 jit_solution(9703437709959540505)
XLA Ops:
  7.4 2.4 broadcast_in_dim.12
  9.8 8.6 %all-to-all-start = ((bf16[32,512,64]{1,2,0:T(8,128)(2,1)}), bf16[32,512,64]{1,2,0:T(8,128)(2,1)S(1)}, u32[]{:S(2)}, u32[]{:S(2)}) async-start(bf16[32,512,64]{1,2,0:T(8,128)(2,1)} %broadcast_in_dim.12), calls=%async_computation | async-start | bytes 4194304 | tf_op jit(solution)/shard_map/all_to_all | solution.py:9
  18.5 28.3 %all-to-all-done = bf16[32,512,64]{1,2,0:T(8,128)(2,1)S(1)} async-done(((bf16[32,512,64]{1,2,0:T(8,128)(2,1)}), bf16[32,512,64]{1,2,0:T(8,128)(2,1)S(1)}, u32[]{:S(2)}, u32[]{:S(2)}) %all-to-all-start) | async-done | bytes 2097184 | tf_op jit(solution)/shard_map/all_to_all | solution.py:9
  46.7 1.1 broadcast_select_fusion
  47.9 1.1 broadcast_select_fusion.1
  49.0 0.7 pad_maximum_fusion.3
  49.8 66.8 %all-reduce.4.cloned.1.call-done = (bf16[64,512]{1,0:T(8,128)(2,1)}, bf16[64,512]{1,0:T(8,128)(2,1)}) async-done(((bf16[64,512]{1,0:T(8,128)(2,1)}, bf16[64,512]{1,0:T(8,128)(2,1)}), (bf16[64,512]{1,0:T(8,128)(2,1)}, bf16[64,512]{1,0:T(8,128)(2,1)})) %all-reduce.4.cloned.1.call-update) | async-done | bytes 131088 | tf_op jit(solution)/shard_map/psum | solution.py:38
  116.6 1.5 pad_maximum_fusion.2
  118.5 19.7 %all-gather = bf16[128,2048]{1,0:T(8,128)(2,1)S(1)} all-gather(bf16[16,2048]{1,0:T(8,128)(2,1)S(1)} %copy.13), channel_id=2, replica_groups=mesh['wide'=32,'narrow'=8] {'narrow'}, dimensions={0}, use_global_device_ids=true | all-gather | bytes 589824 | tf_op jit(solution)/shard_map/all_gather | solution.py:24
  138.2 2.0 fusion.1
  140.2 2.0 fusion.34
  142.2 1.1 broadcast_in_dim.28
  143.3 17.3 %all-to-all-start.2 = ((f32[32,16,512]{2,1,0:T(8,128)}), f32[32,16,512]{2,1,0:T(8,128)S(1)}, u32[]{:S(2)}, u32[]{:S(2)}) async-start(f32[32,16,512]{2,1,0:T(8,128)} %broadcast_in_dim.28), calls=%async_computation.2 | async-start | bytes 2097152 | tf_op jit(solution)/shard_map/all_to_all | solution.py:9
  160.7 7.0 %fusion.3 = f32[512,1024]{1,0:T(8,128)} fusion(bf16[1024,2048]{1,0:T(8,128)(2,1)} %param.4, bf16[2048,1024]{1,0:T(8,128)(2,1)} %all-gather.6.cloned.1.call-done), kind=kOutput, calls=%fused_computation.8 | convolution fusion | flops 2147483648 | bytes 8388608 | tf_op jit(solution)/shard_map/dot_general | solution.py:62
  167.6 3.7 %fusion.7 = f32[512,1024]{1,0:T(8,128)} fusion(bf16[1024,2048]{1,0:T(8,128)(2,1)S(1)} %copy-done.9, bf16[2048,1024]{1,0:T(8,128)(2,1)S(1)} %copy-done.2), kind=kOutput, calls=%fused_computation.12 | convolution fusion | flops 2147483648 | bytes 8388608 | tf_op jit(solution)/shard_map/dot_general | solution.py:61
  171.3 9.7 %all-gather.4.cloned.1.call-done = bf16[2048,1024]{1,0:T(8,128)(2,1)} async-done(((bf16[64,1024]{1,0:T(8,128)(2,1)}), bf16[2048,1024]{1,0:T(8,128)(2,1)}) %all-gather.4.cloned.1.call-update) | async-done | bytes 4194320 | tf_op jit(solution)/shard_map/all_gather | solution.py:29
  181.0 2.0 fusion.11
  183.0 2.0 fusion.37
  185.0 1.1 broadcast_in_dim.14
  186.1 6.1 %all-to-all-start.1 = ((f32[32,16,512]{2,1,0:T(8,128)}), f32[32,16,512]{2,1,0:T(8,128)S(1)}, u32[]{:S(2)}, u32[]{:S(2)}) async-start(f32[32,16,512]{2,1,0:T(8,128)} %broadcast_in_dim.14), calls=%async_computation.1 | async-start | bytes 2097152 | tf_op jit(solution)/shard_map/all_to_all | solution.py:9
  192.2 5.3 %fusion.9 = f32[512,1024]{1,0:T(8,128)S(1)} fusion(bf16[1024,2048]{1,0:T(8,128)(2,1)} %param.4, bf16[2048,1024]{1,0:T(8,128)(2,1)} %all-gather.4.cloned.1.call-done), kind=kOutput, calls=%fused_computation.14 | convolution fusion | flops 2147483648 | bytes 8388608 | tf_op jit(solution)/shard_map/dot_general | solution.py:73
  197.6 3.8 %multiply_multiply_fusion = f32[512,1024]{1,0:T(8,128)} fusion(f32[512,1024]{1,0:T(8,128)S(1)} %fusion.9, bf16[1024,2048]{1,0:T(8,128)(2,1)S(1)} %copy-done.10, bf16[2048,1024]{1,0:T(8,128)(2,1)S(1)} %copy-done.1), kind=kOutput, calls=%fused_computation.5 | convolution fusion | flops 2148532224 | bytes 10485760 | tf_op jit(solution)/shard_map/dot_general | solution.py:72
  201.4 1.0 fusion.95
  202.4 6.6 %all-to-all-done.1 = f32[32,16,512]{2,1,0:T(8,128)S(1)} async-done(((f32[32,16,512]{2,1,0:T(8,128)}), f32[32,16,512]{2,1,0:T(8,128)S(1)}, u32[]{:S(2)}, u32[]{:S(2)}) %all-to-all-start.1) | async-done | bytes 1048608 | tf_op jit(solution)/shard_map/all_to_all | solution.py:9
  209.6 11.7 %cholesky.104 = f32[128,128]{1,0:T(8,128)S(1)} custom-call(f32[128,128]{1,0:T(8,128)S(1)} %cholesky.266), custom_call_target="Cholesky" | custom-call | tf_op jit(solution)/shard_map/jit(cholesky)/cholesky | solution.py:79
  221.4 9.8 %custom-call.34 = f32[1,128,128]{1,2,0:T(8,128)S(1)} custom-call(f32[1,128,128]{2,1,0:T(8,128)S(1)} %get-tuple-element.38), custom_call_target="InvertDiagBlocksLowerTriangular" | custom-call | tf_op jit(solution)/shard_map/jit(cholesky)/cholesky | solution.py:79
  232.1 11.7 %cholesky.217 = f32[128,128]{1,0:T(8,128)S(1)} custom-call(f32[128,128]{1,0:T(8,128)S(1)} %cholesky.270), custom_call_target="Cholesky" | custom-call | tf_op jit(solution)/shard_map/jit(cholesky)/cholesky | solution.py:79
  243.9 9.8 %custom-call.35 = f32[1,128,128]{1,2,0:T(8,128)S(1)} custom-call(f32[1,128,128]{2,1,0:T(8,128)S(1)} %get-tuple-element.35), custom_call_target="InvertDiagBlocksLowerTriangular" | custom-call | tf_op jit(solution)/shard_map/jit(cholesky)/cholesky | solution.py:79
  254.4 11.7 %cholesky.238 = f32[128,128]{1,0:T(8,128)S(1)} custom-call(f32[128,128]{1,0:T(8,128)S(1)} %cholesky.275), custom_call_target="Cholesky" | custom-call | tf_op jit(solution)/shard_map/jit(cholesky)/cholesky | solution.py:79
  266.1 0.7 compare_reduce_fusion.1
  266.8 10.2 %custom-call.36 = f32[1,128,128]{1,2,0:T(8,128)S(1)} custom-call(f32[1,128,128]{2,1,0:T(8,128)S(1)} %get-tuple-element.32), custom_call_target="InvertDiagBlocksLowerTriangular" | custom-call | tf_op jit(solution)/shard_map/jit(cholesky)/cholesky | solution.py:79
  277.6 11.7 %cholesky.255 = f32[128,128]{1,0:T(8,128)S(1)} custom-call(f32[128,128]{1,0:T(8,128)S(1)} %convolution_subtract_fusion.7), custom_call_target="Cholesky" | custom-call | tf_op jit(solution)/shard_map/jit(cholesky)/cholesky | solution.py:79
  289.4 0.7 compare_reduce_fusion
  290.1 0.7 compare_reduce_fusion.2
  293.6 10.7 %while.1 = (s32[]{:T(128)}, f32[512,512]{1,0:T(8,128)S(1)}, s32[4,2]{0,1:T(2,128)S(1)}, f32[4,128,128]{2,1,0:T(8,128)}, s32[]{:T(128)}) while((s32[]{:T(128)}, f32[512,512]{1,0:T(8,128)S(1)}, s32[4,2]{0,1:T(2,128)S(1)}, f32[4,128,128]{2,1,0:T(8,128)}, s32[]{:T(128)}) %tuple.32), condition=%wide.while_cond, body=%wide.while_body.sunk | while | flops 2 | bytes 132705 | solution.py:80
  294.3 2.0 bitcast_dynamic-update-slice_fusion.2
  296.9 2.0 bitcast_dynamic-update-slice_fusion.2
  299.6 2.0 bitcast_dynamic-update-slice_fusion.2
  302.3 2.0 bitcast_dynamic-update-slice_fusion.2
  304.3 40.3 %custom-call.37 = f32[4,128,128]{1,2,0:T(8,128)S(1)} custom-call(f32[4,128,128]{2,1,0:T(8,128)} %get-tuple-element.12), custom_call_target="InvertDiagBlocksLowerTriangular" | custom-call | tf_op jit(solution)/shard_map/jit(_solve_triangular)/triangular_solve | solution.py:80
  346.8 0.6 convolution_subtract_fusion.4
  347.9 0.6 fusion.56
  349.1 0.6 fusion.78
  349.7 0.7 convolution_subtract_fusion
  350.5 0.6 fusion.80
  351.1 1.1 fusion.25
  352.9 4.0 %fusion = f32[1024,512]{0,1:T(8,128)S(1)} fusion(f32[512,1024]{1,0:T(8,128)S(1)} %copy-done.12, f32[512,1024]{1,0:T(8,128)S(1)} %copy-done.11, f32[128,1024]{1,0:T(8,128)S(1)} %fusion.82, f32[128,1024]{1,0:T(8,128)S(1)} %fusion.80, f32[128,1024]{1,0:T(8,128)S(1)} %fusion.78, f32[128,1024]{1,0:T(8,128)S(1)} %fusion.56, f32[128,512]{1,0:T(8,128)S(1)} %fusion.81, ...), kind=kOutput, calls=%fused_computation.4 | convolution fusion | flops 3227254784 | bytes 9437185 | tf_op jit(solution)/shard_map/dot_general | solution.py:82
  356.9 1.8 copy.16
  (72 shorter events, 10.0 us)
Async XLA Ops:
  7.4 39.4 %copy-start = (bf16[64,2048]{1,0:T(8,128)(2,1)S(1)}, bf16[64,2048]{1,0:T(8,128)(2,1)}, u32[]{:S(2)}) copy-start(bf16[64,2048]{1,0:T(8,128)(2,1)} %param.7) | copy-start | bytes 786436
  9.8 36.9 %all-to-all-start = ((bf16[32,512,64]{1,2,0:T(8,128)(2,1)}), bf16[32,512,64]{1,2,0:T(8,128)(2,1)S(1)}, u32[]{:S(2)}, u32[]{:S(2)}) async-start(bf16[32,512,64]{1,2,0:T(8,128)(2,1)} %broadcast_in_dim.12), calls=%async_computation | async-start | bytes 4194304 | tf_op jit(solution)/shard_map/all_to_all | solution.py:9
  18.4 29.5 %copy-start.8 = (bf16[64,2048]{1,0:T(8,128)(2,1)S(1)}, bf16[64,2048]{1,0:T(8,128)(2,1)}, u32[]{:S(2)}) copy-start(bf16[64,2048]{1,0:T(8,128)(2,1)} %param.6) | copy-start | bytes 786436
  18.4 98.2 %all-reduce.4.cloned.1.call-start = ((), (), s32[]{:S(2)}) async-start(), calls=%async_computation.5 | async-start | bytes 262144 | tf_op jit(solution)/shard_map/psum | solution.py:38
  49.0 89.3 %all-gather.6.cloned.1.call-start = ((), (), s32[]{:S(2)}) async-start(), calls=%async_computation.4 | async-start | bytes 4325376 | tf_op jit(solution)/shard_map/all_gather | solution.py:29
  49.7 131.3 %all-gather.4.cloned.1.call-start = ((), (), s32[]{:S(2)}) async-start(), calls=%async_computation.3 | async-start | bytes 4325376 | tf_op jit(solution)/shard_map/all_gather | solution.py:29
  143.3 41.7 %all-to-all-start.2 = ((f32[32,16,512]{2,1,0:T(8,128)}), f32[32,16,512]{2,1,0:T(8,128)S(1)}, u32[]{:S(2)}, u32[]{:S(2)}) async-start(f32[32,16,512]{2,1,0:T(8,128)} %broadcast_in_dim.28), calls=%async_computation.2 | async-start | bytes 2097152 | tf_op jit(solution)/shard_map/all_to_all | solution.py:9
  160.7 7.0 %copy-start.2 = (bf16[2048,1024]{1,0:T(8,128)(2,1)S(1)}, bf16[2048,1024]{1,0:T(8,128)(2,1)}, u32[]{:S(2)}) copy-start(bf16[2048,1024]{1,0:T(8,128)(2,1)} %all-gather.6.cloned.1.call-done) | copy-start | bytes 12582916
  160.7 7.0 %copy-start.9 = (bf16[1024,2048]{1,0:T(8,128)(2,1)S(1)}, bf16[1024,2048]{1,0:T(8,128)(2,1)}, u32[]{:S(2)}) copy-start(bf16[1024,2048]{1,0:T(8,128)(2,1)} %param.4) | copy-start | bytes 12582916
  186.1 22.9 %all-to-all-start.1 = ((f32[32,16,512]{2,1,0:T(8,128)}), f32[32,16,512]{2,1,0:T(8,128)S(1)}, u32[]{:S(2)}, u32[]{:S(2)}) async-start(f32[32,16,512]{2,1,0:T(8,128)} %broadcast_in_dim.14), calls=%async_computation.1 | async-start | bytes 2097152 | tf_op jit(solution)/shard_map/all_to_all | solution.py:9
  192.2 5.4 %copy-start.1 = (bf16[2048,1024]{1,0:T(8,128)(2,1)S(1)}, bf16[2048,1024]{1,0:T(8,128)(2,1)}, u32[]{:S(2)}) copy-start(bf16[2048,1024]{1,0:T(8,128)(2,1)} %all-gather.4.cloned.1.call-done) | copy-start | bytes 12582916
  192.2 5.4 %copy-start.10 = (bf16[1024,2048]{1,0:T(8,128)(2,1)S(1)}, bf16[1024,2048]{1,0:T(8,128)(2,1)}, u32[]{:S(2)}) copy-start(bf16[1024,2048]{1,0:T(8,128)(2,1)} %param.4) | copy-start | bytes 12582916
  254.3 90.3 %copy-start.5 = (f32[8,16,512]{2,1,0:T(8,128)S(1)}, f32[8,16,512]{2,1,0:T(8,128)}, u32[]{:S(2)}) copy-start(f32[8,16,512]{2,1,0:T(8,128)} %get-tuple-element.25) | copy-start | bytes 786436
  277.0 68.1 %copy-start.4 = (f32[8,16,512]{2,1,0:T(8,128)S(1)}, f32[8,16,512]{2,1,0:T(8,128)}, u32[]{:S(2)}) copy-start(f32[8,16,512]{2,1,0:T(8,128)} %get-tuple-element.28) | copy-start | bytes 786436
  293.4 52.5 %copy-start.7 = (f32[8,16,512]{2,1,0:T(8,128)S(1)}, f32[8,16,512]{2,1,0:T(8,128)}, u32[]{:S(2)}) copy-start(f32[8,16,512]{2,1,0:T(8,128)} %get-tuple-element.27) | copy-start | bytes 786436
  304.3 42.5 %copy-start.6 = (f32[8,16,512]{2,1,0:T(8,128)S(1)}, f32[8,16,512]{2,1,0:T(8,128)}, u32[]{:S(2)}) copy-start(f32[8,16,512]{2,1,0:T(8,128)} %get-tuple-element.26) | copy-start | bytes 786436
  345.5 2.4 copy-start.3
  350.5 2.4 copy-start.12
  351.1 1.8 copy-start.11
Sparse Core Ops, SparseCore 0:
  49.1 67.4 all-reduce.3
Sparse Core Ops, SparseCore 1:
  52.0 50.4 all-gather.5
  118.2 62.8 all-gather.3
where the time goes:
time: 373 us; the launch traced here: 366 us
  other arithmetic  122 us (33%)
  waiting for transfers between devices  111 us (30%)
  matrix products  43.9 us (12%)
  starting transfers between devices  32.2 us (9%)
  blocking collectives  19.7 us (5%)
  local copies, waits for them, and re-layouts  19.1 us (5%)
  between operations  18.1 us (5%)
    another operation x14, other arithmetic, per_device(): factor = jnp.linalg.cholesky(diag_block)  78.9 us
    psum x1, waiting for transfers between devices, spread(): return lax.psum(kept, axis)  66.8 us
    another operation x3, other arithmetic, per_device(): jax.scipy.linalg.solve_triangular(factor, slab_first.T, lower=True)  40.5 us
    all_to_all x3, waiting for transfers between devices, from_everyone(): lax.all_to_all(jnp.broadcast_to(x[None], (devices, *x.shape)), axis, 0, 0...  34.9 us
    all_to_all x3, starting transfers between devices, from_everyone(): lax.all_to_all(jnp.broadcast_to(x[None], (devices, *x.shape)), axis, 0, 0...  32 us
    all_gather x1, blocking collectives, broadcast(): lax.all_gather(x, axis)  19.7 us
    dot_general x2, matrix products, per_device(): jnp.dot(row_slice, pieces[1], preferred_element_type=jnp.float32)  12.3 us
    another operation x12, local copies, waits for them, and re-layouts  10.7 us
  transfers between devices with their start and end apart: 6, of which 4 were waited for; matrix products, arithmetic and copies ran while one was open for 9% of the time, Pallas kernels for 0%

commit v1 on v0

--- a/solution.py
+++ b/solution.py
@@ -2,6 +2,8 @@
 import jax.numpy as jnp
 from jax import lax
 from jax.sharding import PartitionSpec as P
+
+wrap_the_keys = lambda across, t0: lax.all_gather(t0, across).sum(axis=0)
 
 
 def from_everyone(x, axis):
@@ -35,7 +37,7 @@
 
 def spread(value, axis, source):
     kept = jnp.where(lax.axis_index(axis) == source, value, 0).astype(value.dtype)
-    return lax.psum(kept, axis)
+    return wrap_the_keys(axis, t0=kept)
 
 
 def per_device(row_vectors, col_vectors, primal_matrix, dual_inverse):

time: 373 us -> 394 us (1.056)
  blocking collectives: 19.7 us -> 61.4 us
  starting transfers between devices: 32.2 us -> 19.8 us
  waiting for transfers between devices: 111 us -> 106 us
    all_gather x2, waiting for transfers between devices: 9.7 us -> 78.1 us  [in_one_piece(): lax.all_gather(both, axis, axis=dim, tiled=True)]
    psum x1 -> x0, waiting for transfers between devices: 66.8 us -> none  [spread(): return lax.psum(kept, axis)]
    all_gather x0 -> x2, blocking collectives: none -> 42 us  [wrap_the_keys = lambda across, t0: lax.all_gather(t0, across).sum(axis=0)]
    all_to_all x3, starting transfers between devices: 32 us -> 19.7 us  [from_everyone(): lax.all_to_all(jnp.broadcast_to(x[None], (devices, *x.shape)), axis, 0, 0...]
    all_to_all x3, waiting for transfers between devices: 34.9 us -> 28.3 us  [from_everyone(): lax.all_to_all(jnp.broadcast_to(x[None], (devices, *x.shape)), axis, 0, 0...]
  transfers between devices with their start and end apart: 6 -> 5, of which waited for: 4 -> 3; matrix products, arithmetic and copies ran while one was open for 9% -> 42% of each run, Pallas kernels for 0% -> 0%
where the time goes in v1:
time: 394 us; the launch traced here: 390 us
  other arithmetic  122 us (31%)
  waiting for transfers between devices  106 us (27%)
  blocking collectives  61.4 us (16%)
  matrix products  43.8 us (11%)
  local copies, waits for them, and re-layouts  20 us (5%)
  starting transfers between devices  19.8 us (5%)
  between operations  16.6 us (4%)
    another operation x14, other arithmetic, per_device(): factor = jnp.linalg.cholesky(diag_block)  78.8 us
    all_gather x2, waiting for transfers between devices, in_one_piece(): lax.all_gather(both, axis, axis=dim, tiled=True)  78.1 us
    all_gather x2, blocking collectives, wrap_the_keys = lambda across, t0: lax.all_gather(t0, across).sum(axis=0)  42 us
    another operation x3, other arithmetic, per_device(): jax.scipy.linalg.solve_triangular(factor, slab_first.T, lower=True)  40.3 us
    all_to_all x3, waiting for transfers between devices, from_everyone(): lax.all_to_all(jnp.broadcast_to(x[None], (devices, *x.shape)), axis, 0, 0...  28.3 us
    all_to_all x3, starting transfers between devices, from_everyone(): lax.all_to_all(jnp.broadcast_to(x[None], (devices, *x.shape)), axis, 0, 0...  19.7 us
    all_gather x1, blocking collectives, broadcast(): lax.all_gather(x, axis)  19.4 us
    dot_general x2, matrix products, per_device(): jnp.dot(row_slice, pieces[1], preferred_element_type=jnp.float32)  13.2 us
  transfers between devices with their start and end apart: 5, of which 3 were waited for; matrix products, arithmetic and copies ran while one was open for 42% of the time, Pallas kernels for 0%

profile of v1, /device:TPU:1, one launch (start us, length us, event | category | flops | bytes accessed | tf_op | source)
XLA Modules:
  0.0 390.1 jit_solution(17799929784607261935)
XLA Ops:
  6.5 2.4 broadcast_in_dim.12
  9.0 8.6 %all-to-all-start = ((bf16[32,512,64]{1,2,0:T(8,128)(2,1)}), bf16[32,512,64]{1,2,0:T(8,128)(2,1)S(1)}, u32[]{:S(2)}, u32[]{:S(2)}) async-start(bf16[32,512,64]{1,2,0:T(8,128)(2,1)} %broadcast_in_dim.12), calls=%async_computation | async-start | bytes 4194304 | tf_op jit(solution)/shard_map/all_to_all | solution.py:11
  17.6 28.3 %all-to-all-done = bf16[32,512,64]{1,2,0:T(8,128)(2,1)S(1)} async-done(((bf16[32,512,64]{1,2,0:T(8,128)(2,1)}), bf16[32,512,64]{1,2,0:T(8,128)(2,1)S(1)}, u32[]{:S(2)}, u32[]{:S(2)}) %all-to-all-start) | async-done | bytes 2097184 | tf_op jit(solution)/shard_map/all_to_all | solution.py:11
  46.4 23.1 %all-gather.1 = bf16[512,512]{1,0:T(8,128)(2,1)S(1)} all-gather(bf16[64,512]{1,0:T(8,128)(2,1)S(1)} %get-tuple-element.39), channel_id=3, replica_groups=mesh['wide'=32,'narrow'=8] {'narrow'}, dimensions={0}, use_global_device_ids=true | all-gather | bytes 589824 | tf_op jit(solution)/shard_map/all_gather | solution.py:6
  70.0 18.9 %all-gather.2 = bf16[512,512]{1,0:T(8,128)(2,1)S(1)} all-gather(bf16[64,512]{1,0:T(8,128)(2,1)S(1)} %get-tuple-element.37), channel_id=4, replica_groups=mesh['wide'=32,'narrow'=8] {'narrow'}, dimensions={0}, use_global_device_ids=true | all-gather | bytes 589824 | tf_op jit(solution)/shard_map/all_gather | solution.py:6
  88.9 0.7 reduce_sum.24
  89.7 1.5 pad_maximum_fusion.2
  91.2 0.7 pad_maximum_fusion.3
  92.4 19.4 %all-gather = bf16[128,2048]{1,0:T(8,128)(2,1)S(1)} all-gather(bf16[16,2048]{1,0:T(8,128)(2,1)S(1)} %copy.13), channel_id=2, replica_groups=mesh['wide'=32,'narrow'=8] {'narrow'}, dimensions={0}, use_global_device_ids=true | all-gather | bytes 589824 | tf_op jit(solution)/shard_map/all_gather | solution.py:26
  111.8 38.6 %all-gather.6.cloned.1.call-done = bf16[2048,1024]{1,0:T(8,128)(2,1)} async-done(((bf16[64,1024]{1,0:T(8,128)(2,1)}), bf16[2048,1024]{1,0:T(8,128)(2,1)}) %all-gather.6.cloned.1.call-update) | async-done | bytes 4194320 | tf_op jit(solution)/shard_map/all_gather | solution.py:31
  150.4 2.0 fusion.11
  152.3 2.0 fusion.37
  154.3 1.2 broadcast_in_dim.14
  155.5 5.6 %all-to-all-start.1 = ((f32[32,16,512]{2,1,0:T(8,128)}), f32[32,16,512]{2,1,0:T(8,128)S(1)}, u32[]{:S(2)}, u32[]{:S(2)}) async-start(f32[32,16,512]{2,1,0:T(8,128)} %broadcast_in_dim.14), calls=%async_computation.1 | async-start | bytes 2097152 | tf_op jit(solution)/shard_map/all_to_all | solution.py:11
  161.1 6.5 %fusion.9 = f32[512,1024]{1,0:T(8,128)} fusion(bf16[1024,2048]{1,0:T(8,128)(2,1)} %param.4, bf16[2048,1024]{1,0:T(8,128)(2,1)} %all-gather.6.cloned.1.call-done), kind=kOutput, calls=%fused_computation.14 | convolution fusion | flops 2147483648 | bytes 8388608 | tf_op jit(solution)/shard_map/dot_general | solution.py:75
  167.6 39.5 %all-gather.8.cloned.1.call-done = bf16[2048,1024]{1,0:T(8,128)(2,1)} async-done(((bf16[64,1024]{1,0:T(8,128)(2,1)}), bf16[2048,1024]{1,0:T(8,128)(2,1)}) %all-gather.8.cloned.1.call-update) | async-done | bytes 4194320 | tf_op jit(solution)/shard_map/all_gather | solution.py:31
  207.1 6.7 %fusion.3 = f32[512,1024]{1,0:T(8,128)} fusion(bf16[1024,2048]{1,0:T(8,128)(2,1)} %param.4, bf16[2048,1024]{1,0:T(8,128)(2,1)} %all-gather.8.cloned.1.call-done), kind=kOutput, calls=%fused_computation.8 | convolution fusion | flops 2147483648 | bytes 8388608 | tf_op jit(solution)/shard_map/dot_general | solution.py:64
  213.8 3.7 fusion.7
  218.3 1.4 copy-done.1
  219.7 3.7 multiply_multiply_fusion
  223.4 1.1 broadcast_in_dim.28
  224.5 5.5 %all-to-all-start.2 = ((f32[32,16,512]{2,1,0:T(8,128)}), f32[32,16,512]{2,1,0:T(8,128)S(1)}, u32[]{:S(2)}, u32[]{:S(2)}) async-start(f32[32,16,512]{2,1,0:T(8,128)} %broadcast_in_dim.28), calls=%async_computation.2 | async-start | bytes 2097152 | tf_op jit(solution)/shard_map/all_to_all | solution.py:11
  230.6 1.0 copy-done.3
  231.6 11.7 %cholesky.104 = f32[128,128]{1,0:T(8,128)S(1)} custom-call(f32[128,128]{1,0:T(8,128)S(1)} %cholesky.266), custom_call_target="Cholesky" | custom-call | tf_op jit(solution)/shard_map/jit(cholesky)/cholesky | solution.py:81
  243.5 9.8 %custom-call.34 = f32[1,128,128]{1,2,0:T(8,128)S(1)} custom-call(f32[1,128,128]{2,1,0:T(8,128)S(1)} %get-tuple-element.36), custom_call_target="InvertDiagBlocksLowerTriangular" | custom-call | tf_op jit(solution)/shard_map/jit(cholesky)/cholesky | solution.py:81
  253.3 1.2 constant_dynamic-update-slice_fusion.3
  254.6 1.3 convolution_subtract_fusion.5
  255.8 11.7 %cholesky.217 = f32[128,128]{1,0:T(8,128)S(1)} custom-call(f32[128,128]{1,0:T(8,128)S(1)} %cholesky.270), custom_call_target="Cholesky" | custom-call | tf_op jit(solution)/shard_map/jit(cholesky)/cholesky | solution.py:81
  267.6 10.2 %custom-call.35 = f32[1,128,128]{1,2,0:T(8,128)S(1)} custom-call(f32[1,128,128]{2,1,0:T(8,128)S(1)} %get-tuple-element.33), custom_call_target="InvertDiagBlocksLowerTriangular" | custom-call | tf_op jit(solution)/shard_map/jit(cholesky)/cholesky | solution.py:81
  278.1 1.3 convolution_subtract_fusion.6
  279.4 11.7 %cholesky.238 = f32[128,128]{1,0:T(8,128)S(1)} custom-call(f32[128,128]{1,0:T(8,128)S(1)} %cholesky.275), custom_call_target="Cholesky" | custom-call | tf_op jit(solution)/shard_map/jit(cholesky)/cholesky | solution.py:81
  291.2 0.7 compare_reduce_fusion.1
  291.8 9.8 %custom-call.36 = f32[1,128,128]{1,2,0:T(8,128)S(1)} custom-call(f32[1,128,128]{2,1,0:T(8,128)S(1)} %get-tuple-element.30), custom_call_target="InvertDiagBlocksLowerTriangular" | custom-call | tf_op jit(solution)/shard_map/jit(cholesky)/cholesky | solution.py:81
  301.8 1.2 convolution_subtract_fusion.7
  303.1 11.7 %cholesky.255 = f32[128,128]{1,0:T(8,128)S(1)} custom-call(f32[128,128]{1,0:T(8,128)S(1)} %convolution_subtract_fusion.7), custom_call_target="Cholesky" | custom-call | tf_op jit(solution)/shard_map/jit(cholesky)/cholesky | solution.py:81
  314.8 0.6 compare_reduce_fusion
  315.5 0.6 compare_reduce_fusion.2
  318.8 10.1 %while.1 = (s32[]{:T(128)}, f32[512,512]{1,0:T(8,128)S(1)}, s32[4,2]{0,1:T(2,128)S(1)}, f32[4,128,128]{2,1,0:T(8,128)}, s32[]{:T(128)}) while((s32[]{:T(128)}, f32[512,512]{1,0:T(8,128)S(1)}, s32[4,2]{0,1:T(2,128)S(1)}, f32[4,128,128]{2,1,0:T(8,128)}, s32[]{:T(128)}) %tuple.32), condition=%wide.while_cond, body=%wide.while_body.sunk | while | flops 2 | bytes 132705 | solution.py:82
  319.4 1.9 bitcast_dynamic-update-slice_fusion.2
  321.9 1.9 bitcast_dynamic-update-slice_fusion.2
  324.5 1.9 bitcast_dynamic-update-slice_fusion.2
  327.0 1.9 bitcast_dynamic-update-slice_fusion.2
  328.9 40.1 %custom-call.37 = f32[4,128,128]{1,2,0:T(8,128)S(1)} custom-call(f32[4,128,128]{2,1,0:T(8,128)} %get-tuple-element.12), custom_call_target="InvertDiagBlocksLowerTriangular" | custom-call | tf_op jit(solution)/shard_map/jit(_solve_triangular)/triangular_solve | solution.py:82
  371.2 0.6 convolution_subtract_fusion.4
  374.2 0.7 convolution_subtract_fusion
  375.6 1.1 fusion.25
  377.3 4.0 %fusion = f32[1024,512]{0,1:T(8,128)S(1)} fusion(f32[512,1024]{1,0:T(8,128)S(1)} %copy-done.8, f32[512,1024]{1,0:T(8,128)S(1)} %copy-done.7, f32[128,1024]{1,0:T(8,128)S(1)} %fusion.82, f32[128,1024]{1,0:T(8,128)S(1)} %fusion.80, f32[128,1024]{1,0:T(8,128)S(1)} %fusion.78, f32[128,1024]{1,0:T(8,128)S(1)} %fusion.56, f32[128,512]{1,0:T(8,128)S(1)} %fusion.81, ...), kind=kOutput, calls=%fused_computation.4 | convolution fusion | flops 3227254784 | bytes 9437185 | tf_op jit(solution)/shard_map/dot_general | solution.py:84
  381.3 1.8 copy.16
  (67 shorter events, 11.9 us)
Async XLA Ops:
  6.5 39.4 %copy-start = (bf16[64,2048]{1,0:T(8,128)(2,1)S(1)}, bf16[64,2048]{1,0:T(8,128)(2,1)}, u32[]{:S(2)}) copy-start(bf16[64,2048]{1,0:T(8,128)(2,1)} %param.6) | copy-start | bytes 786436
  9.0 36.9 %all-to-all-start = ((bf16[32,512,64]{1,2,0:T(8,128)(2,1)}), bf16[32,512,64]{1,2,0:T(8,128)(2,1)S(1)}, u32[]{:S(2)}, u32[]{:S(2)}) async-start(bf16[32,512,64]{1,2,0:T(8,128)(2,1)} %broadcast_in_dim.12), calls=%async_computation | async-start | bytes 4194304 | tf_op jit(solution)/shard_map/all_to_all | solution.py:11
  17.6 52.0 %copy-start.5 = (bf16[64,2048]{1,0:T(8,128)(2,1)S(1)}, bf16[64,2048]{1,0:T(8,128)(2,1)}, u32[]{:S(2)}) copy-start(bf16[64,2048]{1,0:T(8,128)(2,1)} %param.7) | copy-start | bytes 786436
  17.6 132.8 %all-gather.6.cloned.1.call-start = ((), (), s32[]{:S(2)}) async-start(), calls=%async_computation.3 | async-start | bytes 4325376 | tf_op jit(solution)/shard_map/all_gather | solution.py:31
  91.2 115.9 %all-gather.8.cloned.1.call-start = ((), (), s32[]{:S(2)}) async-start(), calls=%async_computation.4 | async-start | bytes 4325376 | tf_op jit(solution)/shard_map/all_gather | solution.py:31
  155.5 67.9 %all-to-all-start.1 = ((f32[32,16,512]{2,1,0:T(8,128)}), f32[32,16,512]{2,1,0:T(8,128)S(1)}, u32[]{:S(2)}, u32[]{:S(2)}) async-start(f32[32,16,512]{2,1,0:T(8,128)} %broadcast_in_dim.14), calls=%async_computation.1 | async-start | bytes 2097152 | tf_op jit(solution)/shard_map/all_to_all | solution.py:11
  207.1 6.7 %copy-start.2 = (bf16[2048,1024]{1,0:T(8,128)(2,1)S(1)}, bf16[2048,1024]{1,0:T(8,128)(2,1)}, u32[]{:S(2)}) copy-start(bf16[2048,1024]{1,0:T(8,128)(2,1)} %all-gather.8.cloned.1.call-done) | copy-start | bytes 12582916
  207.1 6.7 %copy-start.6 = (bf16[1024,2048]{1,0:T(8,128)(2,1)S(1)}, bf16[1024,2048]{1,0:T(8,128)(2,1)}, u32[]{:S(2)}) copy-start(bf16[1024,2048]{1,0:T(8,128)(2,1)} %param.4) | copy-start | bytes 12582916
  213.8 4.5 %copy-start.9 = (f32[512,1024]{1,0:T(8,128)S(1)}, f32[512,1024]{1,0:T(8,128)}, u32[]{:S(2)}) copy-start(f32[512,1024]{1,0:T(8,128)} %fusion.9) | copy-start | bytes 6291460
  217.5 2.2 copy-start.1
  224.5 144.5 %all-to-all-start.2 = ((f32[32,16,512]{2,1,0:T(8,128)}), f32[32,16,512]{2,1,0:T(8,128)S(1)}, u32[]{:S(2)}, u32[]{:S(2)}) async-start(f32[32,16,512]{2,1,0:T(8,128)} %broadcast_in_dim.28), calls=%async_computation.2 | async-start | bytes 2097152 | tf_op jit(solution)/shard_map/all_to_all | solution.py:11
  230.6 1.0 copy-start.3
  369.9 2.4 copy-start.4
  374.9 2.4 copy-start.8
  375.5 1.8 copy-start.7
Sparse Core Ops, SparseCore 0:
  91.3 59.0 all-gather.5
  152.9 54.0 all-gather.7
